TPU v7x, 32 devices: a whole 2x2x4 slice. The times are simulated.
32 devices in a mesh: shard: 8 (over z, x), rep: 4 (over y, core).
Axes of the slice: x: 2, y: 2, z: 4, core: 2. Of those that a mesh axis runs over, the one named last changes fastest.
Arguments:
- lender_block: int32 [96, 8], P(('shard', 'rep')), may hold values from 0 to 255, as said below
- confidence: bfloat16 [96, 8, 256, 256], P(('shard', 'rep')), may hold values from 0 to 80, as said below
- lender_factors: bfloat16 [65536, 128], P('shard'), may hold values from -4 to 4
Outputs:
- borrower_factors: float32 [24576, 128], P(('shard', 'rep'))
- lender_rhs: float32 [65536, 128], P('shard')
Inputs may be any that keep to these rules, and one draw needn't show every extreme that they name: `lender_block`: within one device's 3 borrower blocks, at most 6 of the 3 x 8 entries name blocks of any one owner (block // 32), and on every device some owner is named exactly 6 times. `confidence`: about half the entries are zero; the others are positive.
All inputs are finite; a program needn't handle non-finite values.
Results may differ from a plain program's by a relative error of at most 0.0047.
Values may be sent and summed in bfloat16 or wider, within the bound.
A program may use at most 128 MiB of HBM per device.

v0:
```python
import jax
import jax.numpy as jnp
from jax import lax
from jax.sharding import PartitionSpec as P

CG_STEPS = 3
HIGH = lax.Precision.HIGHEST


def apply_system(direction, confidence, fetched, gram):
    low = direction.astype(jnp.bfloat16)
    scores = jnp.einsum("btr,bklr->bktl", low, fetched, preferred_element_type=jnp.float32)
    weighted = (confidence.astype(jnp.float32) * scores).astype(jnp.bfloat16)
    back = jnp.einsum("bktl,bklr->btr", weighted, fetched, preferred_element_type=jnp.float32)
    width = direction.shape[-1]
    global_part = jnp.dot(
        direction.reshape(-1, width), gram, precision=HIGH, preferred_element_type=jnp.float32
    )
    return global_part.reshape(direction.shape) + 0.1 * direction + back


WIRE = jnp.float16
TOP = 14.0
EXTRA = 16


def encode(value):
    largest = jnp.maximum(jnp.max(jnp.abs(value)), 1e-30)
    level = jnp.ceil(jnp.log2(largest))
    return ((value * jnp.exp2(TOP - level)).astype(WIRE), level)


def with_level(chunks, level):
    head = jnp.broadcast_to(level.astype(WIRE), (chunks.shape[0], EXTRA, chunks.shape[2]))
    return jnp.concatenate([chunks, head], axis=1)


def decode(packed, rows):
    level = packed[:, rows : rows + 1, :1].astype(jnp.float32)
    return packed[:, :rows].astype(jnp.float32) * jnp.exp2(level - TOP)


def per_device(lender_block, confidence, lender_factors):
    shards = lax.axis_size("shard")
    blocks, lists = lender_block.shape
    tile = confidence.shape[2]
    rank = lender_factors.shape[1]
    owned = lender_factors.shape[0] // tile
    entries = blocks * lists
    slots = (2 * entries + shards - 1) // shards
    reps = lax.axis_size("rep")
    me = lax.axis_index("shard")
    part = tile // reps
    local_gram = lax.dot_general(
        lender_factors, lender_factors, (((0,), (0,)), ((), ())), preferred_element_type=jnp.float32
    )
    flat = lender_block.reshape(entries)
    listed = lax.all_gather(flat, ("shard", "rep"), axis=0, tiled=False)
    mine = (listed // owned == me).astype(jnp.int32)
    place = jnp.cumsum(mine, axis=1) - 1
    slot_ids = jnp.arange(slots, dtype=jnp.int32)
    hit = (place[:, :, None] == slot_ids) & (mine[:, :, None] == 1)
    within = listed - owned * me
    named = jnp.sum(jnp.where(hit, within[:, :, None] + 1, 0), axis=1) - 1
    owner = flat // owned
    member = (owner[:, None] == jnp.arange(shards, dtype=jnp.int32)[None, :]).astype(jnp.int32)
    position = jnp.sum(jnp.cumsum(member, axis=0) * member, axis=1) - 1
    slot_index = owner * slots + position
    table = lender_factors.reshape(owned, tile, rank)
    incoming = lax.dynamic_index_in_dim(
        named.reshape(shards, reps, slots), lax.axis_index("rep"), axis=1, keepdims=False
    )
    wanted = table[jnp.maximum(incoming, 0)]
    wanted, local_gram = lax.optimization_barrier((wanted, local_gram))
    gram = lax.psum(local_gram, "shard")
    replies = lax.all_to_all(wanted, "shard", split_axis=0, concat_axis=0, tiled=True)
    fetched = replies.reshape(shards * slots, tile, rank)[slot_index].reshape(
        blocks, lists, tile, rank
    )
    rhs = jnp.einsum("bktl,bklr->btr", confidence, fetched, preferred_element_type=jnp.float32)
    solution = jnp.zeros_like(rhs)
    resid = rhs
    direction = rhs
    norm_now = jnp.sum(resid * resid, axis=2, keepdims=True)
    for count in range(CG_STEPS):
        image = apply_system(direction, confidence, fetched, gram)
        alpha = norm_now / (jnp.sum(direction * image, axis=2, keepdims=True) + 1e-06)
        solution = solution + alpha * direction
        resid = resid - alpha * image
        norm_next = jnp.sum(resid * resid, axis=2, keepdims=True)
        direction = resid + norm_next / (norm_now + 1e-06) * direction
        norm_now = norm_next
    solved = solution.astype(jnp.bfloat16)
    partial_rhs = jnp.einsum(
        "bktl,btr->bklr", confidence, solved, preferred_element_type=jnp.float32
    )
    coded, level = encode(partial_rhs)
    every = jnp.arange(shards * slots, dtype=jnp.int32)
    source = jnp.argmax(slot_index[None, :] == every[:, None], axis=1).astype(jnp.int32)
    quarter = jnp.arange(reps, dtype=jnp.int32)
    pick = source.reshape(shards, 1, slots) * reps + quarter[None, :, None]
    chunks = coded.reshape(entries * reps, part, rank)[pick.reshape(-1)]
    chunks = chunks.reshape(shards * reps, slots * part, rank)
    outgoing = with_level(chunks, level)
    returned = lax.all_to_all(outgoing, ("shard", "rep"), split_axis=0, concat_axis=0, tiled=True)
    back = decode(returned, slots * part)
    selector = (named.reshape(-1)[None, :] == jnp.arange(owned, dtype=jnp.int32)[:, None]).astype(
        jnp.float32
    )
    owner_sum = jnp.dot(
        selector,
        back.reshape(shards * reps * slots, part * rank),
        precision=HIGH,
        preferred_element_type=jnp.float32,
    )
    coded, level = encode(owner_sum.reshape(owned * part, rank))
    shared = lax.all_gather(with_level(coded[None], level)[0], "rep", axis=0, tiled=False)
    lenders_all = owned * tile * shards
    total = decode(shared, owned * part) / lenders_all
    lender_rhs = total.reshape(reps, owned, part, rank).transpose(1, 0, 2, 3)
    lender_rhs = lender_rhs.reshape(owned * tile, rank)
    return (solution.reshape(blocks * tile, rank), lender_rhs)


def solution(mesh):
    in_specs = (P(("shard", "rep"), None), P(("shard", "rep"), None, None, None), P("shard", None))
    out_specs = (P(("shard", "rep"), None), P("shard", None))
    return jax.shard_map(
        per_device, mesh=mesh, in_specs=in_specs, out_specs=out_specs, check_vma=False
    )
```

profile of v0, /device:TPU:0, one launch (start us, length us, event | category | flops | bytes accessed | tf_op | source)
XLA Modules:
  0.0 330.6 jit_solution(16797563167929177055)
XLA Ops:
  7.2 0.9 reshape.352
  8.1 43.3 %all-gather = s32[32,1,24]{2,1,0:T(1,128)S(1)} all-gather(s32[1,1,24]{2,1,0:T(1,128)S(1)} %reshape.352), channel_id=1, replica_groups=mesh['shard'=8,'rep'=4] {'shard','rep'}, dimensions={0}, use_global_device_ids=true | all-gather | bytes 3168 | tf_op jit(solution)/shard_map/all_gather | solution.py:58
  52.3 1.4 fusion.62
  53.7 2.7 gather_fusion
  56.4 4.6 %all-to-all-start = ((bf16[8,6,256,128]{3,2,1,0:T(8,128)(2,1)}), bf16[8,6,256,128]{3,2,1,0:T(8,128)(2,1)}, u32[]{:S(2)}, u32[]{:S(2)}) async-start(bf16[8,6,256,128]{3,2,1,0:T(8,128)(2,1)} %bitcast.109), calls=%async_computation | async-start | bytes 6291456 | tf_op jit(solution)/shard_map/all_to_all | solution.py:76
  63.0 4.7 %copy.162 = bf16[3,8,256,256]{2,3,1,0:T(8,128)(2,1)} copy(bf16[3,8,256,256]{3,2,1,0:T(8,128)(2,1)} %param.4) | data formatting | bytes 6291456 | tf_op args[1]
  67.7 66.2 %all-to-all-done = bf16[8,6,256,128]{3,2,1,0:T(8,128)(2,1)} async-done(((bf16[8,6,256,128]{3,2,1,0:T(8,128)(2,1)}), bf16[8,6,256,128]{3,2,1,0:T(8,128)(2,1)}, u32[]{:S(2)}, u32[]{:S(2)}) %all-to-all-start) | async-done | bytes 3145760 | tf_op jit(solution)/shard_map/all_to_all | solution.py:76
  133.9 3.8 %gather_fusion.1 = bf16[24,256,128]{2,1,0:T(8,128)(2,1)} fusion(bf16[48,256,128]{2,1,0:T(8,128)(2,1)} %bitcast.3, s32[1024]{0:T(1024)S(1)} %pad_clamp_fusion.1), kind=kCustom, calls=%fused_computation.1 | custom fusion | bytes 3145824 | tf_op jit(solution)/shard_map/gather | solution.py:77
  137.7 3.5 %convolution_bitcast_fusion = f32[3,256,128]{1,2,0:T(8,128)S(1)} fusion(bf16[3,8,256,128]{3,2,1,0:T(8,128)(2,1)} %bitcast.111, bf16[3,8,256,256]{3,2,1,0:T(8,128)(2,1)} %param.4), kind=kOutput, calls=%fused_computation.26 | convolution fusion | flops 402653184 | bytes 5111808 | tf_op jit(solution)/shard_map/bktl,bklr->btr/dot_general | solution.py:80
  141.3 4.3 %fusion.16 = f32[3,256,128]{1,2,0:T(8,128)S(1)} fusion(bf16[3,8,256,128]{3,2,1,0:T(8,128)(2,1)} %bitcast.112, bf16[3,8,256,256]{2,3,1,0:T(8,128)(2,1)} %copy.162, f32[3,256,128]{1,2,0:T(8,128)S(1)} %convolution_bitcast_fusion), kind=kOutput, calls=%fused_computation.20 | convolution fusion | flops 810123264 | bytes 5505024 | tf_op jit(solution)/shard_map/bktl,bklr->btr/dot_general | solution.py:14
  145.6 20.3 %all-reduce.4.cloned.1.call-done = f32[128,128]{1,0:T(8,128)} async-done(((f32[128,128]{1,0:T(8,128)}), f32[128,128]{1,0:T(8,128)}) %all-reduce.4.cloned.1.call-update) | async-done | bytes 65552 | tf_op jit(solution)/shard_map/psum | solution.py:75
  165.9 1.4 multiply_reduce_fusion.3
  167.5 5.1 %fusion.19 = f32[3,256,128]{1,2,0:T(8,128)} fusion(bf16[3,8,256,128]{3,2,1,0:T(8,128)(2,1)} %bitcast.113, bf16[3,8,256,256]{2,3,1,0:T(8,128)(2,1)} %copy.162, f32[3,256,128]{1,2,0:T(8,128)S(1)} %multiply_add_fusion.2), kind=kOutput, calls=%fused_computation.21 | convolution fusion | flops 810123264 | bytes 5505024 | tf_op jit(solution)/shard_map/bktl,bklr->btr/dot_general | solution.py:14
  172.6 1.6 multiply_reduce_fusion.1
  175.1 5.2 %fusion.22 = f32[3,256,128]{1,2,0:T(8,128)} fusion(bf16[3,8,256,128]{3,2,1,0:T(8,128)(2,1)} %bitcast.114, bf16[3,8,256,256]{2,3,1,0:T(8,128)(2,1)} %copy.162, f32[3,256,128]{1,2,0:T(8,128)} %multiply_add_fusion.1), kind=kOutput, calls=%fused_computation.22 | convolution fusion | flops 810123264 | bytes 5505024 | tf_op jit(solution)/shard_map/bktl,bklr->btr/dot_general | solution.py:14
  180.2 1.6 fusion.29
  181.8 1.1 multiply_add_fusion
  182.9 4.7 %abs_reduce_fusion = (f32[]{:T(128)}, f32[3,128,8,256]{3,1,2,0:T(8,128)}) fusion(bf16[3,8,256,256]{3,2,1,0:T(8,128)(2,1)} %param.4, f32[3,256,128]{1,2,0:T(8,128)S(1)} %multiply_add_fusion), kind=kOutput, calls=%fused_computation.15 | convolution fusion | flops 404324352 | bytes 6684676 | tf_op jit(solution)/shard_map/bktl,btr->bklr/dot_general | solution.py:94
  188.4 3.5 %fusion.15 = f16[3,8,256,128]{2,3,1,0:T(8,128)(2,1)} fusion(f32[3,128,8,256]{3,1,2,0:T(8,128)} %get-tuple-element.18, f32[]{:T(128)S(6)} %exp2.28), kind=kLoop, calls=%fused_computation.19 | loop fusion | flops 1572864 | bytes 4718596 | tf_op jit(solution)/shard_map/convert_element_type | solution.py:30
  191.9 3.0 copy.178
  194.9 4.8 %gather_fusion.2 = f16[192,64,128]{2,1,0:T(8,128)(2,1)} fusion(f16[96,64,128]{2,1,0:T(8,128)(2,1)} %bitcast.108, s32[1024]{0:T(1024)S(1)} %pad_clamp_fusion), kind=kCustom, calls=%fused_computation.2 | custom fusion | bytes 6292224 | tf_op jit(solution)/shard_map/gather | solution.py:102
  199.7 4.2 %concatenate.6 = f16[32,400,128]{2,1,0:T(8,128)(2,1)} pad(f16[32,384,128]{2,1,0:T(8,128)(2,1)} %bitcast.110, f16[]{:T(256)S(6)} %convert_element_type.82), padding=0_0x0_16x0_0 | pad | bytes 6422530 | tf_op jit(solution)/shard_map/concatenate | solution.py:35
  203.9 4.8 %all-to-all-start.1 = ((f16[32,400,128]{2,1,0:T(8,128)(2,1)}), f16[32,400,128]{2,1,0:T(8,128)(2,1)}, u32[]{:S(2)}, u32[]{:S(2)}) async-start(f16[32,400,128]{2,1,0:T(8,128)(2,1)} %concatenate.6), calls=%async_computation.1 | async-start | bytes 6553600 | tf_op jit(solution)/shard_map/all_to_all | solution.py:105
  208.9 0.9 copy.176
  209.9 73.1 %all-to-all-done.1 = f16[32,400,128]{2,1,0:T(8,128)(2,1)} async-done(((f16[32,400,128]{2,1,0:T(8,128)(2,1)}), f16[32,400,128]{2,1,0:T(8,128)(2,1)}, u32[]{:S(2)}, u32[]{:S(2)}) %all-to-all-start.1) | async-done | bytes 3276832 | tf_op jit(solution)/shard_map/all_to_all | solution.py:105
  284.0 5.3 %convert_multiply_fusion.3 = f32[32,384,128]{2,1,0:T(8,128)} fusion(f16[32,400,128]{2,1,0:T(8,128)(2,1)} %all-to-all-done.1, f32[32]{0:T(128)S(1)} %exponential_bitcast_fusion), kind=kLoop, calls=%fused_computation.9 | loop fusion | flops 3145728 | bytes 9437312 | tf_op jit(solution)/shard_map/mul | solution.py:40
  289.3 7.2 %reshape.323 = f32[192,8192]{1,0:T(8,128)} reshape(f32[32,384,128]{2,1,0:T(8,128)} %convert_multiply_fusion.3) | data formatting | bytes 12582912 | tf_op jit(solution)/shard_map/reshape | solution.py:112
  296.4 5.9 %abs_reduce_fusion.1 = (f32[]{:T(128)}, f32[32,8192]{1,0:T(8,128)S(1)}) fusion(f32[192,8192]{1,0:T(8,128)} %reshape.323, s32[192]{0:T(256)S(1)} %sub.66), kind=kOutput, calls=%fused_computation.33 | convolution fusion | flops 604510208 | bytes 7340804 | tf_op jit(solution)/shard_map/dot_general | solution.py:110
  303.1 0.9 multiply_convert_fusion.1
  304.0 1.3 convert_element_type.86
  305.5 15.4 %all-gather.2 = f16[4,2064,128]{2,1,0:T(8,128)(2,1)S(1)} all-gather(f16[1,2064,128]{2,1,0:T(8,128)(2,1)S(1)} %concatenate.7), channel_id=1, replica_groups=mesh['shard'=8,'rep'=4] {'rep'}, dimensions={0}, use_global_device_ids=true | all-gather | bytes 2641920 | tf_op jit(solution)/shard_map/all_gather | solution.py:117
  321.5 2.3 copy.180
  (57 shorter events, 5.8 us)
Async XLA Ops:
  7.2 45.1 %copy-start = (bf16[8192,128]{1,0:T(8,128)(2,1)S(1)}, bf16[8192,128]{1,0:T(8,128)(2,1)}, u32[]{:S(2)}) copy-start(bf16[8192,128]{1,0:T(8,128)(2,1)} %param.5) | copy-start | bytes 6291460
  56.4 5.3 %copy-start.3 = (s32[3,8]{1,0:T(4,128)S(1)}, s32[3,8]{1,0:T(4,128)}, u32[]{:S(2)}) copy-start(s32[3,8]{1,0:T(4,128)} %param.3) | copy-start | bytes 292
  56.4 77.5 %all-to-all-start = ((bf16[8,6,256,128]{3,2,1,0:T(8,128)(2,1)}), bf16[8,6,256,128]{3,2,1,0:T(8,128)(2,1)}, u32[]{:S(2)}, u32[]{:S(2)}) async-start(bf16[8,6,256,128]{3,2,1,0:T(8,128)(2,1)} %bitcast.109), calls=%async_computation | async-start | bytes 6291456 | tf_op jit(solution)/shard_map/all_to_all | solution.py:76
  60.9 104.9 %all-reduce.4.cloned.1.call-start = ((), (), s32[]{:S(2)}) async-start(), calls=%async_computation.2 | async-start | bytes 131072 | tf_op jit(solution)/shard_map/psum | solution.py:75
  167.5 5.1 %copy-start.2 = (f32[128,128]{1,0:T(8,128)S(1)}, f32[128,128]{1,0:T(8,128)}, u32[]{:S(2)}) copy-start(f32[128,128]{1,0:T(8,128)} %all-reduce.4.cloned.1.call-done) | copy-start | bytes 196612
  175.1 5.2 %copy-start.1 = (f32[3,256,128]{1,2,0:T(8,128)S(1)}, f32[3,256,128]{1,2,0:T(8,128)}, u32[]{:S(2)}) copy-start(f32[3,256,128]{1,2,0:T(8,128)} %multiply_add_fusion.1) | copy-start | bytes 1179652
  203.9 79.1 %all-to-all-start.1 = ((f16[32,400,128]{2,1,0:T(8,128)(2,1)}), f16[32,400,128]{2,1,0:T(8,128)(2,1)}, u32[]{:S(2)}, u32[]{:S(2)}) async-start(f16[32,400,128]{2,1,0:T(8,128)(2,1)} %concatenate.6), calls=%async_computation.1 | async-start | bytes 6553600 | tf_op jit(solution)/shard_map/all_to_all | solution.py:105
Sparse Core Ops, SparseCore 0:
  65.7 100.0 all-reduce.3
where the time goes:
time: 332 us; the launch traced here: 331 us
  waiting for transfers between devices  160 us (48%)
  blocking collectives  58.7 us (18%)
  local copies, waits for them, and re-layouts  38.1 us (11%)
  matrix products  34.7 us (10%)
  between operations  15.7 us (5%)
  other arithmetic  13.7 us (4%)
  starting transfers between devices  9.45 us (3%)
    all_to_all x1, waiting for transfers between devices, per_device(): lax.all_to_all(outgoing, ('shard', 'rep'), split_axis=0, concat_axis=0, t...  73.1 us
    all_to_all x1, waiting for transfers between devices, per_device(): lax.all_to_all(wanted, 'shard', split_axis=0, concat_axis=0, tiled=True)  66.2 us
    all_gather x1, blocking collectives, per_device(): listed = lax.all_gather(flat, ('shard', 'rep'), axis=0, tiled=False)  43.3 us
    psum x1, waiting for transfers between devices, per_device(): gram = lax.psum(local_gram, 'shard')  20.3 us
    all_gather x1, blocking collectives, per_device(): lax.all_gather(with_level(coded[None], level)[0], 'rep', axis=0, tiled=Fa...  15.4 us
    dot_general x3, matrix products, apply_system(): jnp.einsum('bktl,bklr->btr', weighted, fetched, preferred_element_type=jn...  14.5 us
    reshape x1, local copies, waits for them, and re-layouts, per_device(): back.reshape(shards * reps * slots, part * rank)  7.15 us
  transfers between devices with their start and end apart: 3, of which 3 were waited for; matrix products, arithmetic and copies ran while one was open for 6% of the time, Pallas kernels for 0%

commit v1 on v0

--- a/solution.py
+++ b/solution.py
@@ -72,7 +72,7 @@
     )
     wanted = table[jnp.maximum(incoming, 0)]
     wanted, local_gram = lax.optimization_barrier((wanted, local_gram))
-    gram = lax.psum(local_gram, "shard")
+    gram = jnp.sum(lax.all_gather(local_gram, "shard"), axis=0)
     replies = lax.all_to_all(wanted, "shard", split_axis=0, concat_axis=0, tiled=True)
     fetched = replies.reshape(shards * slots, tile, rank)[slot_index].reshape(
         blocks, lists, tile, rank

time: 332 us -> 315 us (0.949)
  waiting for transfers between devices: 160 us -> 73.3 us
  blocking collectives: 58.7 us -> 145 us
  between operations: 15.7 us -> 2.37 us
    all_gather x0 -> x1, blocking collectives: none -> 86.5 us  [per_device(): gram = jnp.sum(lax.all_gather(local_gram, 'shard'), axis=0)]
    all_to_all x1, waiting for transfers between devices: 66.2 us -> 0.01 us  [per_device(): lax.all_to_all(wanted, 'shard', split_axis=0, concat_axis=0, tiled=True)]
    psum x1 -> x0, waiting for transfers between devices: 20.3 us -> none  [per_device(): gram = lax.psum(local_gram, 'shard')]
  transfers between devices with their start and end apart: 3 -> 2, of which waited for: 3 -> 1; matrix products, arithmetic and copies ran while one was open for 6% -> 2% of each run, Pallas kernels for 0% -> 0%
where the time goes in v1:
time: 315 us; the launch traced here: 314 us
  blocking collectives  145 us (46%)
  waiting for transfers between devices  73.3 us (23%)
  local copies, waits for them, and re-layouts  38 us (12%)
  matrix products  33.2 us (11%)
  other arithmetic  13.8 us (4%)
  starting transfers between devices  8.33 us (3%)
    all_gather x1, blocking collectives, per_device(): gram = jnp.sum(lax.all_gather(local_gram, 'shard'), axis=0)  86.5 us
    all_to_all x1, waiting for transfers between devices, per_device(): lax.all_to_all(outgoing, ('shard', 'rep'), split_axis=0, concat_axis=0, t...  73.3 us
    all_gather x1, blocking collectives, per_device(): listed = lax.all_gather(flat, ('shard', 'rep'), axis=0, tiled=False)  43.3 us
    all_gather x1, blocking collectives, per_device(): lax.all_gather(with_level(coded[None], level)[0], 'rep', axis=0, tiled=Fa...  15.3 us
    dot_general x3, matrix products, apply_system(): jnp.einsum('bktl,bklr->btr', weighted, fetched, preferred_element_type=jn...  14.5 us
    reshape x1, local copies, waits for them, and re-layouts, per_device(): back.reshape(shards * reps * slots, part * rank)  7.15 us
  transfers between devices with their start and end apart: 2, of which 1 were waited for; matrix products, arithmetic and copies ran while one was open for 2% of the time, Pallas kernels for 0%

profile of v1, /device:TPU:0, one launch (start us, length us, event | category | flops | bytes accessed | tf_op | source)
XLA Modules:
  0.0 314.1 jit_solution(11973449196371604702)
XLA Ops:
  0.6 0.9 reshape.353
  1.6 43.3 %all-gather.1 = s32[32,1,24]{2,1,0:T(1,128)S(1)} all-gather(s32[1,1,24]{2,1,0:T(1,128)S(1)} %reshape.353), channel_id=1, replica_groups=mesh['shard'=8,'rep'=4] {'shard','rep'}, dimensions={0}, use_global_device_ids=true | all-gather | bytes 3168 | tf_op jit(solution)/shard_map/all_gather | solution.py:58
  45.7 0.7 fusion.62
  46.5 2.7 gather_fusion
  49.2 4.6 %all-to-all-start = ((bf16[8,6,256,128]{3,2,1,0:T(8,128)(2,1)}), bf16[8,6,256,128]{3,2,1,0:T(8,128)(2,1)}, u32[]{:S(2)}, u32[]{:S(2)}) async-start(bf16[8,6,256,128]{3,2,1,0:T(8,128)(2,1)} %bitcast.110), calls=%async_computation | async-start | bytes 6291456 | tf_op jit(solution)/shard_map/all_to_all | solution.py:76
  55.1 4.7 %copy.165 = bf16[3,8,256,256]{2,3,1,0:T(8,128)(2,1)} copy(bf16[3,8,256,256]{3,2,1,0:T(8,128)(2,1)} %param.4) | data formatting | bytes 6291456 | tf_op args[1]
  59.8 86.5 %all-gather = f32[1024,128]{1,0:T(8,128)S(1)} all-gather(f32[128,128]{1,0:T(8,128)S(1)} %fusion.62), channel_id=2, replica_groups=mesh['shard'=8,'rep'=4] {'shard'}, dimensions={0}, use_global_device_ids=true | all-gather | bytes 589824 | tf_op jit(solution)/shard_map/all_gather | solution.py:75
  146.5 3.8 %gather_fusion.1 = bf16[24,256,128]{2,1,0:T(8,128)(2,1)} fusion(bf16[48,256,128]{2,1,0:T(8,128)(2,1)} %bitcast.3, s32[1024]{0:T(1024)S(1)} %pad_clamp_fusion.1), kind=kCustom, calls=%fused_computation.1 | custom fusion | bytes 3145824 | tf_op jit(solution)/shard_map/gather | solution.py:77
  150.3 3.5 %convolution_bitcast_fusion = f32[3,256,128]{1,2,0:T(8,128)S(1)} fusion(bf16[3,8,256,128]{3,2,1,0:T(8,128)(2,1)} %bitcast.112, bf16[3,8,256,256]{3,2,1,0:T(8,128)(2,1)} %param.4), kind=kOutput, calls=%fused_computation.26 | convolution fusion | flops 402653184 | bytes 5111808 | tf_op jit(solution)/shard_map/bktl,bklr->btr/dot_general | solution.py:80
  153.8 4.3 %fusion.16 = f32[3,256,128]{1,2,0:T(8,128)S(1)} fusion(bf16[3,8,256,128]{3,2,1,0:T(8,128)(2,1)} %bitcast.113, bf16[3,8,256,256]{2,3,1,0:T(8,128)(2,1)} %copy.165, f32[3,256,128]{1,2,0:T(8,128)S(1)} %convolution_bitcast_fusion), kind=kOutput, calls=%fused_computation.20 | convolution fusion | flops 810123264 | bytes 5505024 | tf_op jit(solution)/shard_map/bktl,bklr->btr/dot_general | solution.py:14
  158.9 5.0 %fusion.19 = f32[3,256,128]{1,2,0:T(8,128)} fusion(bf16[3,8,256,128]{3,2,1,0:T(8,128)(2,1)} %bitcast.114, bf16[3,8,256,256]{2,3,1,0:T(8,128)(2,1)} %copy.165, f32[3,256,128]{1,2,0:T(8,128)S(1)} %multiply_add_fusion.2), kind=kOutput, calls=%fused_computation.21 | convolution fusion | flops 810123264 | bytes 5505024 | tf_op jit(solution)/shard_map/bktl,bklr->btr/dot_general | solution.py:14
  163.9 1.6 multiply_reduce_fusion.1
  165.6 0.8 multiply_add_fusion.1
  166.4 5.2 %fusion.22 = f32[3,256,128]{1,2,0:T(8,128)} fusion(bf16[3,8,256,128]{3,2,1,0:T(8,128)(2,1)} %bitcast.115, bf16[3,8,256,256]{2,3,1,0:T(8,128)(2,1)} %copy.165, f32[3,256,128]{1,2,0:T(8,128)} %multiply_add_fusion.1), kind=kOutput, calls=%fused_computation.22 | convolution fusion | flops 810123264 | bytes 5505024 | tf_op jit(solution)/shard_map/bktl,bklr->btr/dot_general | solution.py:14
  171.6 1.6 fusion.29
  173.2 1.1 multiply_add_fusion
  174.3 4.7 %abs_reduce_fusion = (f32[]{:T(128)}, f32[3,128,8,256]{3,1,2,0:T(8,128)}) fusion(bf16[3,8,256,256]{3,2,1,0:T(8,128)(2,1)} %param.4, f32[3,256,128]{1,2,0:T(8,128)S(1)} %multiply_add_fusion), kind=kOutput, calls=%fused_computation.15 | convolution fusion | flops 404324352 | bytes 6684676 | tf_op jit(solution)/shard_map/bktl,btr->bklr/dot_general | solution.py:94
  179.8 3.5 %fusion.15 = f16[3,8,256,128]{2,3,1,0:T(8,128)(2,1)} fusion(f32[3,128,8,256]{3,1,2,0:T(8,128)} %get-tuple-element.18, f32[]{:T(128)S(6)} %exp2.28), kind=kLoop, calls=%fused_computation.19 | loop fusion | flops 1572864 | bytes 4718596 | tf_op jit(solution)/shard_map/convert_element_type | solution.py:30
  183.3 3.0 copy.181
  186.2 4.8 %gather_fusion.2 = f16[192,64,128]{2,1,0:T(8,128)(2,1)} fusion(f16[96,64,128]{2,1,0:T(8,128)(2,1)} %bitcast.109, s32[1024]{0:T(1024)S(1)} %pad_clamp_fusion), kind=kCustom, calls=%fused_computation.2 | custom fusion | bytes 6292224 | tf_op jit(solution)/shard_map/gather | solution.py:102
  191.0 4.2 %concatenate.6 = f16[32,400,128]{2,1,0:T(8,128)(2,1)} pad(f16[32,384,128]{2,1,0:T(8,128)(2,1)} %bitcast.111, f16[]{:T(256)S(6)} %convert_element_type.82), padding=0_0x0_16x0_0 | pad | bytes 6422530 | tf_op jit(solution)/shard_map/concatenate | solution.py:35
  195.3 3.8 %all-to-all-start.1 = ((f16[32,400,128]{2,1,0:T(8,128)(2,1)}), f16[32,400,128]{2,1,0:T(8,128)(2,1)}, u32[]{:S(2)}, u32[]{:S(2)}) async-start(f16[32,400,128]{2,1,0:T(8,128)(2,1)} %concatenate.6), calls=%async_computation.1 | async-start | bytes 6553600 | tf_op jit(solution)/shard_map/all_to_all | solution.py:105
  199.2 0.9 copy.179
  200.2 73.3 %all-to-all-done.1 = f16[32,400,128]{2,1,0:T(8,128)(2,1)} async-done(((f16[32,400,128]{2,1,0:T(8,128)(2,1)}), f16[32,400,128]{2,1,0:T(8,128)(2,1)}, u32[]{:S(2)}, u32[]{:S(2)}) %all-to-all-start.1) | async-done | bytes 3276832 | tf_op jit(solution)/shard_map/all_to_all | solution.py:105
  273.4 0.9 slice.23
  274.4 5.3 %convert_multiply_fusion.3 = f32[32,384,128]{2,1,0:T(8,128)} fusion(f16[32,400,128]{2,1,0:T(8,128)(2,1)} %all-to-all-done.1, f32[32]{0:T(128)S(1)} %exponential_bitcast_fusion), kind=kLoop, calls=%fused_computation.9 | loop fusion | flops 3145728 | bytes 9437312 | tf_op jit(solution)/shard_map/mul | solution.py:40
  279.7 7.2 %reshape.323 = f32[192,8192]{1,0:T(8,128)} reshape(f32[32,384,128]{2,1,0:T(8,128)} %convert_multiply_fusion.3) | data formatting | bytes 12582912 | tf_op jit(solution)/shard_map/reshape | solution.py:112
  286.9 5.9 %abs_reduce_fusion.1 = (f32[]{:T(128)}, f32[32,8192]{1,0:T(8,128)S(1)}) fusion(f32[192,8192]{1,0:T(8,128)} %reshape.323, s32[192]{0:T(256)S(1)} %sub.66), kind=kOutput, calls=%fused_computation.33 | convolution fusion | flops 604510208 | bytes 7340804 | tf_op jit(solution)/shard_map/dot_general | solution.py:110
  293.5 0.9 multiply_convert_fusion.1
  294.4 1.3 convert_element_type.86
  295.9 15.3 %all-gather.3 = f16[4,2064,128]{2,1,0:T(8,128)(2,1)S(1)} all-gather(f16[1,2064,128]{2,1,0:T(8,128)(2,1)S(1)} %concatenate.7), channel_id=1, replica_groups=mesh['shard'=8,'rep'=4] {'rep'}, dimensions={0}, use_global_device_ids=true | all-gather | bytes 2641920 | tf_op jit(solution)/shard_map/all_gather | solution.py:117
  311.7 2.3 copy.183
  (54 shorter events, 4.1 us)
Async XLA Ops:
  0.6 45.1 %copy-start = (bf16[8192,128]{1,0:T(8,128)(2,1)S(1)}, bf16[8192,128]{1,0:T(8,128)(2,1)}, u32[]{:S(2)}) copy-start(bf16[8192,128]{1,0:T(8,128)(2,1)} %param.5) | copy-start | bytes 6291460
  49.2 4.6 %copy-start.2 = (s32[3,8]{1,0:T(4,128)S(1)}, s32[3,8]{1,0:T(4,128)}, u32[]{:S(2)}) copy-start(s32[3,8]{1,0:T(4,128)} %param.3) | copy-start | bytes 292
  49.2 97.2 %all-to-all-start = ((bf16[8,6,256,128]{3,2,1,0:T(8,128)(2,1)}), bf16[8,6,256,128]{3,2,1,0:T(8,128)(2,1)}, u32[]{:S(2)}, u32[]{:S(2)}) async-start(bf16[8,6,256,128]{3,2,1,0:T(8,128)(2,1)} %bitcast.110), calls=%async_computation | async-start | bytes 6291456 | tf_op jit(solution)/shard_map/all_to_all | solution.py:76
  166.4 5.2 %copy-start.1 = (f32[3,256,128]{1,2,0:T(8,128)S(1)}, f32[3,256,128]{1,2,0:T(8,128)}, u32[]{:S(2)}) copy-start(f32[3,256,128]{1,2,0:T(8,128)} %multiply_add_fusion.1) | copy-start | bytes 1179652
  195.3 78.1 %all-to-all-start.1 = ((f16[32,400,128]{2,1,0:T(8,128)(2,1)}), f16[32,400,128]{2,1,0:T(8,128)(2,1)}, u32[]{:S(2)}, u32[]{:S(2)}) async-start(f16[32,400,128]{2,1,0:T(8,128)(2,1)} %concatenate.6), calls=%async_computation.1 | async-start | bytes 6553600 | tf_op jit(solution)/shard_map/all_to_all | solution.py:105
